TPU v7x, 32 devices: a whole 2x2x4 slice. The times are simulated.
32 devices in a mesh: rows: 8 (over y, x, core), rep: 4 (over z).
Axes of the slice: x: 2, y: 2, z: 4, core: 2. Of those that a mesh axis runs over, the one named last changes fastest.
Arguments:
- maps: float32 [4, 4096, 4096], P('rep', 'rows'), may hold values from -12 to 12
- mask: int32 [4096, 4096], P('rows'), may hold values 0 or 1
- bins: int32 [4096, 4096], P(None, 'rows'), may hold values from 0 to 1023
Outputs:
- spectra: float32 [2, 3, 1024], replicated
All inputs are finite; a program needn't handle non-finite values. No bound on the sum of `mask` on one device may be relied on, other than what follows from the above.
Results may differ from a plain program's by a relative error of at most 0.0016.
Values sent between devices are 32-bit elements; how exact they have to be, the bound alone decides.
No kernel may reach another device: no remote copies, remote signals or barrier semaphores. Data moves between devices by JAX's collectives and lax.ppermute only.
A program may use at most 128 MiB of HBM per device.

v0:
```python
import math
import jax
import jax.numpy as jnp
from jax import lax
from jax.sharding import PartitionSpec as P

NBINS = 1024
precise = lax.Precision.HIGHEST


def partner(array, axis, distance):
    return lax.ppermute(array, axis, [(i, i ^ 1 << distance) for i in range(lax.axis_size(axis))])


def dft_table(count_a, count_b, period):
    first = lax.iota(jnp.int32, count_a)[:, None]
    second = lax.iota(jnp.int32, count_b)[None, :]
    angles = (first * second % period).astype(jnp.float32) * (2.0 * math.pi / period)
    return (jnp.cos(angles), -jnp.sin(angles))


def split_length(length):
    outer_len = 2 ** ((length.bit_length() - 1) // 2)
    return (outer_len, length // outer_len)


def complex_apply(form, real_part, imag_part, table_cos, table_sin):

    def product(left, right):
        return jnp.einsum(form, left, right, precision=precise)

    return (
        product(real_part, table_cos) - product(imag_part, table_sin),
        product(real_part, table_sin) + product(imag_part, table_cos),
    )


def twiddled(real_part, imag_part, table_cos, table_sin):
    return (
        real_part * table_cos - imag_part * table_sin,
        real_part * table_sin + imag_part * table_cos,
    )


def row_transform(values):
    count, length = values.shape
    outer_len, inner_len = split_length(length)
    outer_cos, outer_sin = dft_table(outer_len, outer_len, outer_len)
    inner_cos, inner_sin = dft_table(inner_len, inner_len, inner_len)
    turn_cos, turn_sin = dft_table(outer_len, inner_len, length)
    shaped = values.reshape(count, outer_len, inner_len)
    first_real = jnp.einsum("yan,ak->ykn", shaped, outer_cos, precision=precise)
    first_imag = jnp.einsum("yan,ak->ykn", shaped, outer_sin, precision=precise)
    mid_real, mid_imag = twiddled(first_real, first_imag, turn_cos, turn_sin)
    last_real, last_imag = complex_apply("ykn,nm->ymk", mid_real, mid_imag, inner_cos, inner_sin)
    return (last_real.reshape(count, length), last_imag.reshape(count, length))


def column_transform(pieces):
    real_part, imag_part = pieces
    length, groups, width = real_part.shape
    outer_len, inner_len = split_length(length)
    outer_cos, outer_sin = dft_table(outer_len, outer_len, outer_len)
    inner_cos, inner_sin = dft_table(inner_len, inner_len, inner_len)
    turn_cos, turn_sin = dft_table(outer_len, inner_len, length)
    shaped_real = real_part.reshape(outer_len, inner_len, groups, width)
    shaped_imag = imag_part.reshape(outer_len, inner_len, groups, width)
    first_real, first_imag = complex_apply(
        "anbc,ak->knbc", shaped_real, shaped_imag, outer_cos, outer_sin
    )
    mid_real, mid_imag = twiddled(
        first_real, first_imag, turn_cos[:, :, None, None], turn_sin[:, :, None, None]
    )
    last_real, last_imag = complex_apply("knbc,nm->mkbc", mid_real, mid_imag, inner_cos, inner_sin)
    return (last_real.reshape(length, groups, width), last_imag.reshape(length, groups, width))


def signed_float(indices, extent):
    return jnp.where(indices >= extent // 2, indices - extent, indices).astype(jnp.float32)


def band_terms(fields, freq_y, freq_x, bin_block, nbins_count, extent):
    q_real, q_imag, u_real, u_imag = fields
    radius = jnp.maximum(freq_x * freq_x + freq_y * freq_y, 1.0)
    cos_twice = (freq_x * freq_x - freq_y * freq_y) / radius
    sin_twice = 2.0 * freq_x * freq_y / radius
    e_real = cos_twice * q_real + sin_twice * u_real
    e_imag = cos_twice * q_imag + sin_twice * u_imag
    b_real = -sin_twice * q_real + cos_twice * u_real
    b_imag = -sin_twice * q_imag + cos_twice * u_imag
    inv_area = 1.0 / (extent * extent)
    powers = jnp.stack(
        [
            (e_real * e_real + e_imag * e_imag) * inv_area,
            (b_real * b_real + b_imag * b_imag) * inv_area,
            (e_real * b_real + e_imag * b_imag) * inv_area,
        ]
    ).astype(jnp.bfloat16)
    bit_count = nbins_count.bit_length() - 1
    high_count = 2 ** max(bit_count // 2 - 1, 0)
    low_count = nbins_count // high_count
    high_part = bin_block // low_count
    low_part = bin_block % low_count
    high_hot = (high_part[None] == lax.iota(jnp.int32, high_count)[:, None, None]).astype(
        jnp.bfloat16
    )
    weighted = (powers[:, None] * high_hot[None]).reshape(3 * high_count, -1)
    low_hot = (low_part[None] == lax.iota(jnp.int32, low_count)[:, None, None]).astype(jnp.bfloat16)
    low_hot = low_hot.reshape(low_count, -1)
    sums = lax.dot_general(
        weighted, low_hot, (((1,), (1,)), ((), ())), preferred_element_type=jnp.float32
    )
    return sums.reshape(3, nbins_count)


def on_device(maps, mask, bins):
    extent = bins.shape[0]
    columns = bins.shape[1]
    count = maps.shape[1]
    slab_index = lax.axis_index("rows")
    member = lax.axis_index("rep")
    pair_bit = member % 2
    field = maps[0] * mask.astype(jnp.float32)
    row_real, row_imag = row_transform(field)
    half_rows = extent // 2
    slabs = (
        row_real.reshape(count, extent // columns, columns),
        row_imag.reshape(count, extent // columns, columns),
    )
    spec_real, spec_imag = column_transform(
        (
            lax.all_to_all(slabs[0], "rows", split_axis=1, concat_axis=0, tiled=True),
            lax.all_to_all(slabs[1], "rows", split_axis=1, concat_axis=0, tiled=True),
        )
    )
    spec_real = spec_real.reshape(extent, columns)
    spec_imag = spec_imag.reshape(extent, columns)
    kept_real = lax.dynamic_slice_in_dim(spec_real, pair_bit * half_rows, half_rows, 0)
    kept_imag = lax.dynamic_slice_in_dim(spec_imag, pair_bit * half_rows, half_rows, 0)
    sent_real = lax.dynamic_slice_in_dim(spec_real, (1 - pair_bit) * half_rows, half_rows, 0)
    sent_imag = lax.dynamic_slice_in_dim(spec_imag, (1 - pair_bit) * half_rows, half_rows, 0)
    got_real, got_imag = partner((sent_real, sent_imag), "rep", 0)
    is_first = pair_bit == 0
    fields = (
        jnp.where(is_first, kept_real, got_real),
        jnp.where(is_first, kept_imag, got_imag),
        jnp.where(is_first, got_real, kept_real),
        jnp.where(is_first, got_imag, kept_imag),
    )
    own_bins = lax.dynamic_slice_in_dim(bins, pair_bit * half_rows, half_rows, 0)

    def frequency_of(offset, height):
        rows_here = lax.iota(jnp.int32, height)[:, None] + offset + pair_bit * half_rows
        cols_here = lax.iota(jnp.int32, columns)[None, :] + slab_index * columns
        return (rows_here, cols_here)

    block = min(256, half_rows)
    blocks = half_rows // block
    stacked = tuple((part.reshape(blocks, block, columns) for part in fields))
    bin_blocks = own_bins.reshape(blocks, block, columns)

    def accumulate(running, items):
        block_index, parts, bin_block = items
        rows_here, cols_here = frequency_of(block_index * block, block)
        term = band_terms(
            parts,
            signed_float(rows_here, extent),
            signed_float(cols_here, extent),
            bin_block,
            NBINS,
            extent,
        )
        return (running + term, None)

    partial_sums, _ = lax.scan(
        accumulate,
        jnp.zeros((3, NBINS), jnp.float32),
        (lax.iota(jnp.int32, blocks), stacked, bin_blocks),
    )
    sims_count = lax.axis_size("rep") // 2
    slot = (lax.iota(jnp.int32, sims_count) == member // 2).astype(jnp.float32)[:, None, None]
    totals = lax.psum(slot * partial_sums[None], ("rows", "rep"))
    auto = NBINS / (extent * extent)
    cross = math.sqrt(auto)
    factors = jnp.array([auto, auto, cross], jnp.float32)[None, :, None]
    return totals * factors


def solution(mesh):
    in_specs = (P("rep", "rows", None), P("rows", None), P(None, "rows"))
    out_specs = P()
    return jax.shard_map(
        on_device, mesh=mesh, in_specs=in_specs, out_specs=out_specs, check_vma=False
    )
```

profile of v0, /device:TPU:0, one launch (start us, length us, event | category | flops | bytes accessed | tf_op | source)
XLA Modules:
  0.0 1004.3 jit_solution(9013043201485757183)
XLA Ops:
  29.3 17.6 %fusion.37 = f32[64,512,64]{1,0,2:T(8,128)} fusion(f32[512,64,64]{0,2,1:T(8,128)} %bitcast.90), kind=kOutput, calls=%fused_computation.67 | convolution fusion | flops 1610674176 | bytes 16777216 | tf_op jit(solution)/shard_map/yan,ak->ykn/dot_general | solution.py:53
  46.9 21.0 %subtract_bitcast_fusion.1 = (f32[512,64,64]{0,1,2:T(8,128)S(1)}, f32[512,64,64]{0,1,2:T(8,128)}) fusion(f32[64,512,64]{1,0,2:T(8,128)} %fusion.37, f32[64,64]{0,1:T(8,128)S(1)} %get-tuple-element.245, f32[64,64]{0,1:T(8,128)S(1)} %get-tuple-element.246, f32[512,64,64]{0,2,1:T(8,128)} %bitcast.91), kind=kOutput, calls=%fused_computation.42 | convolution fusion | flops 1623252992 | bytes 33587200 | tf_op jit(solution)/shard_map/yan,ak->ykn/dot_general | solution.py:52
  67.9 19.2 %fusion.29 = f32[64,512,64]{1,0,2:T(8,128)S(1)} fusion(f32[512,64,64]{0,1,2:T(8,128)} %get-tuple-element.240), kind=kOutput, calls=%fused_computation.59 | convolution fusion | flops 1610670080 | bytes 16777216 | tf_op jit(solution)/shard_map/ykn,nm->ymk/dot_general | solution.py:30
  117.9 16.3 %fusion.31 = f32[64,512,64]{1,0,2:T(8,128)S(1)} fusion(f32[512,64,64]{0,1,2:T(8,128)} %get-tuple-element.240), kind=kOutput, calls=%fused_computation.61 | convolution fusion | flops 1610674176 | bytes 16777216 | tf_op jit(solution)/shard_map/ykn,nm->ymk/dot_general | solution.py:30
  134.2 17.1 %subtract_bitcast_fusion = f32[512,64,64]{0,1,2:T(8,128)S(1)} fusion(f32[64,512,64]{1,0,2:T(8,128)S(1)} %fusion.31, f32[512,64,64]{0,1,2:T(8,128)} %copy-done), kind=kOutput, calls=%fused_computation.40 | convolution fusion | flops 1612767232 | bytes 25165824 | tf_op jit(solution)/shard_map/ykn,nm->ymk/dot_general | solution.py:30
  159.4 53.0 %all-to-all-done.1 = f32[512,8,512]{0,2,1:T(8,128)} async-done(((f32[512,8,512]{0,2,1:T(8,128)}), f32[512,8,512]{0,2,1:T(8,128)}, u32[]{:S(2)}, u32[]{:S(2)}) %all-to-all-start.1) | async-done | bytes 8388640 | tf_op jit(solution)/shard_map/all_to_all | solution.py:133
  226.9 17.8 %fusion.21 = f32[64,64,512]{2,0,1:T(8,128)} fusion(f32[64,64,512]{2,1,0:T(8,128)} %bitcast.92), kind=kOutput, calls=%fused_computation.51 | convolution fusion | flops 1610670080 | bytes 16777216 | tf_op jit(solution)/shard_map/anbc,ak->knbc/dot_general | solution.py:30
  258.5 53.4 %all-to-all-done = f32[512,8,512]{0,2,1:T(8,128)} async-done(((f32[512,8,512]{0,2,1:T(8,128)}), f32[512,8,512]{0,2,1:T(8,128)}, u32[]{:S(2)}, u32[]{:S(2)}) %all-to-all-start) | async-done | bytes 8388640 | tf_op jit(solution)/shard_map/all_to_all | solution.py:132
  321.0 17.7 %fusion.27 = f32[64,64,512]{2,0,1:T(8,128)} fusion(f32[64,64,512]{2,1,0:T(8,128)} %bitcast.94), kind=kOutput, calls=%fused_computation.57 | convolution fusion | flops 1610670080 | bytes 16777216 | tf_op jit(solution)/shard_map/anbc,ak->knbc/dot_general | solution.py:30
  338.7 24.6 %multiply_subtract_fusion = (f32[64,64,512]{2,0,1:T(8,128)}, f32[64,64,512]{2,0,1:T(8,128)}) fusion(f32[64,64]{0,1:T(8,128)S(1)} %get-tuple-element.245, f32[64,64]{0,1:T(8,128)S(1)} %get-tuple-element.246, f32[64,64,512]{2,0,1:T(8,128)} %fusion.21, f32[64,64,512]{2,0,1:T(8,128)} %fusion.27, f32[64,64,512]{2,0,1:T(8,128)} %fusion.23, ...), kind=kOutput, calls=%fused_computation.38 | convolution fusion | flops 1627451392 | bytes 50364416 | tf_op jit(solution)/shard_map/anbc,ak->knbc/dot_general | solution.py:30
  363.3 18.5 %fusion.13 = f32[64,64,512]{2,0,1:T(8,128)} fusion(f32[64,64,512]{2,0,1:T(8,128)} %get-tuple-element.238), kind=kOutput, calls=%fused_computation.43 | convolution fusion | flops 1610670080 | bytes 16777216 | tf_op jit(solution)/shard_map/knbc,nm->mkbc/dot_general | solution.py:30
  394.3 15.6 %fusion.48 = f32[64,64,512]{2,0,1:T(8,128)} fusion(f32[64,64,512]{2,0,1:T(8,128)} %fusion.13, f32[64,64,512]{2,0,1:T(8,128)S(1)} %bitcast.89), kind=kOutput, calls=%fused_computation.76 | convolution fusion | flops 1612771328 | bytes 25165824 | tf_op jit(solution)/shard_map/knbc,nm->mkbc/dot_general | solution.py:30
  460.7 59.4 %collective-permute-done.1 = f32[2048,512]{1,0:T(8,128)} collective-permute-done((f32[2048,512]{1,0:T(8,128)}, f32[2048,512]{1,0:T(8,128)}, u32[]{:S(2)}, u32[]{:S(2)}) %collective-permute-start.1) | collective-permute-done | bytes 4194336 | tf_op jit(solution)/shard_map/ppermute | solution.py:12
  528.2 78.0 %collective-permute-done = f32[2048,512]{1,0:T(8,128)} collective-permute-done((f32[2048,512]{1,0:T(8,128)}, f32[2048,512]{1,0:T(8,128)}, u32[]{:S(2)}, u32[]{:S(2)}) %collective-permute-start) | collective-permute-done | bytes 4194336 | tf_op jit(solution)/shard_map/ppermute | solution.py:12
  612.8 348.4 %while.14 = (s32[]{:T(128)}, f32[3,1024]{1,0:T(4,128)S(1)}, s32[]{:T(128)}, s32[8]{0:T(128)S(1)}, s32[]{:T(128)}, /*index=5*/f32[8,256,512]{2,1,0:T(8,128)}, f32...) while((s32[]{:T(128)}, f32[3,1024]{1,0:T(4,128)S(1)}, ...), condition=%wide.region_1.2_spmd.clone, body=%wide.region_0.1_spmd.clone.sunk | while | flops 832713472 | bytes 68505800 | solution.py:175
  622.1 28.9 %copy.81 = bf16[6,8,256,512]{3,1,2,0:T(8,128)(2,1)S(1)} copy(bf16[6,8,256,512]{3,2,1,0:T(8,128)(2,1)S(1)} %bitcast.86) | data formatting | bytes 25165824 | tf_op jit(solution)/shard_map/while
  665.6 28.9 %copy.81 = bf16[6,8,256,512]{3,1,2,0:T(8,128)(2,1)S(1)} copy(bf16[6,8,256,512]{3,2,1,0:T(8,128)(2,1)S(1)} %bitcast.86) | data formatting | bytes 25165824 | tf_op jit(solution)/shard_map/while
  709.2 28.9 %copy.81 = bf16[6,8,256,512]{3,1,2,0:T(8,128)(2,1)S(1)} copy(bf16[6,8,256,512]{3,2,1,0:T(8,128)(2,1)S(1)} %bitcast.86) | data formatting | bytes 25165824 | tf_op jit(solution)/shard_map/while
  752.7 28.9 %copy.81 = bf16[6,8,256,512]{3,1,2,0:T(8,128)(2,1)S(1)} copy(bf16[6,8,256,512]{3,2,1,0:T(8,128)(2,1)S(1)} %bitcast.86) | data formatting | bytes 25165824 | tf_op jit(solution)/shard_map/while
  796.2 28.9 %copy.81 = bf16[6,8,256,512]{3,1,2,0:T(8,128)(2,1)S(1)} copy(bf16[6,8,256,512]{3,2,1,0:T(8,128)(2,1)S(1)} %bitcast.86) | data formatting | bytes 25165824 | tf_op jit(solution)/shard_map/while
  839.7 28.9 %copy.81 = bf16[6,8,256,512]{3,1,2,0:T(8,128)(2,1)S(1)} copy(bf16[6,8,256,512]{3,2,1,0:T(8,128)(2,1)S(1)} %bitcast.86) | data formatting | bytes 25165824 | tf_op jit(solution)/shard_map/while
  883.3 28.9 %copy.81 = bf16[6,8,256,512]{3,1,2,0:T(8,128)(2,1)S(1)} copy(bf16[6,8,256,512]{3,2,1,0:T(8,128)(2,1)S(1)} %bitcast.86) | data formatting | bytes 25165824 | tf_op jit(solution)/shard_map/while
  926.8 28.9 %copy.81 = bf16[6,8,256,512]{3,1,2,0:T(8,128)(2,1)S(1)} copy(bf16[6,8,256,512]{3,2,1,0:T(8,128)(2,1)S(1)} %bitcast.86) | data formatting | bytes 25165824 | tf_op jit(solution)/shard_map/while
  961.3 41.8 %psum.7 = f32[2,3,1024]{2,0,1:T(2,128)S(1)} all-reduce(f32[2,3,1024]{2,0,1:T(2,128)S(1)} %broadcast_multiply_fusion.2), channel_id=1, replica_groups=mesh['rows'=8,'rep'=4] {'rows','rep'}, use_global_device_ids=true, to_apply=%region_2.3 | all-reduce | flops 6144 | bytes 49152 | tf_op jit(solution)/shard_map/psum | solution.py:182
  (160 shorter events, 295.2 us)
Async XLA Ops:
  67.9 19.2 %copy-start = (f32[512,64,64]{0,1,2:T(8,128)}, f32[512,64,64]{0,1,2:T(8,128)S(1)}, u32[]{:S(2)}) copy-start(f32[512,64,64]{0,1,2:T(8,128)S(1)} %get-tuple-element.239) | copy-start | bytes 25165828
  112.5 100.0 %all-to-all-start.1 = ((f32[512,8,512]{0,2,1:T(8,128)}), f32[512,8,512]{0,2,1:T(8,128)}, u32[]{:S(2)}, u32[]{:S(2)}) async-start(f32[512,8,512]{0,2,1:T(8,128)} %bitcast.103), calls=%async_computation.1 | async-start | bytes 16777216 | tf_op jit(solution)/shard_map/all_to_all | solution.py:133
  212.4 99.4 %all-to-all-start = ((f32[512,8,512]{0,2,1:T(8,128)}), f32[512,8,512]{0,2,1:T(8,128)}, u32[]{:S(2)}, u32[]{:S(2)}) async-start(f32[512,8,512]{0,2,1:T(8,128)} %bitcast.102), calls=%async_computation | async-start | bytes 16777216 | tf_op jit(solution)/shard_map/all_to_all | solution.py:132
  226.9 17.8 %copy-start.1 = (f32[8,512,1,512]{3,1,0,2:T(8,128)S(1)}, f32[8,512,1,512]{3,1,0,2:T(8,128)}, u32[]{:S(2)}) copy-start(f32[8,512,1,512]{3,1,0,2:T(8,128)} %copy.27) | copy-start | bytes 25165828
  363.3 18.5 %copy-start.2 = (f32[64,64,512]{2,0,1:T(8,128)S(1)}, f32[64,64,512]{2,0,1:T(8,128)}, u32[]{:S(2)}) copy-start(f32[64,64,512]{2,0,1:T(8,128)} %get-tuple-element.238) | copy-start | bytes 25165828
  363.3 31.0 %slice-start = ((s8[8388608]{0:T(1024)(128)(4,1)}), s8[4194304]{0:T(1024)(128)(4,1)S(1)}, s32[]{:S(2)}) async-start(s8[8388608]{0:T(1024)(128)(4,1)} %bitcast.88), calls=%async_computation.2 | async-start | bytes 8388608
  381.8 12.5 %slice-start.1 = ((s8[8388608]{0:T(1024)(128)(4,1)}), s8[4194304]{0:T(1024)(128)(4,1)S(1)}, s32[]{:S(2)}) async-start(s8[8388608]{0:T(1024)(128)(4,1)} %bitcast.88), calls=%async_computation.3 | async-start | bytes 8388608
  426.1 94.0 %collective-permute-start.1 = (f32[2048,512]{1,0:T(8,128)}, f32[2048,512]{1,0:T(8,128)}, u32[]{:S(2)}, u32[]{:S(2)}) collective-permute-start(f32[2048,512]{1,0:T(8,128)} %constant_dynamic-slice_fusion.1), channel_id=1, source_target_pairs={{0,1},{1,0},{2,3},{3,2},{4,5},{5,4},{6,7},{7,6},{8,9},{9,8},{10,11... | collective-permute-start | bytes 12582920 | tf_op jit(solution)/shard_map/ppermute | solution.py:12
  450.2 3.2 copy-start.3
  455.9 150.3 %collective-permute-start = (f32[2048,512]{1,0:T(8,128)}, f32[2048,512]{1,0:T(8,128)}, u32[]{:S(2)}, u32[]{:S(2)}) collective-permute-start(f32[2048,512]{1,0:T(8,128)} %constant_dynamic-slice_fusion.2), channel_id=1, source_target_pairs={{0,1},{1,0},{2,3},{3,2},{4,5},{5,4},{6,7},{7,6},{8,9},{9,8},{10,11... | collective-permute-start | bytes 12582920 | tf_op jit(solution)/shard_map/ppermute | solution.py:12
  455.9 150.3 %slice-start.2 = ((s8[8388608]{0:T(1024)(128)(4,1)}), s8[4194304]{0:T(1024)(128)(4,1)S(1)}, s32[]{:S(2)}) async-start(s8[8388608]{0:T(1024)(128)(4,1)} %bitcast.99), calls=%async_computation.4 | async-start | bytes 8388608
  460.7 145.5 %slice-start.3 = ((s8[8388608]{0:T(1024)(128)(4,1)}), s8[4194304]{0:T(1024)(128)(4,1)S(1)}, s32[]{:S(2)}) async-start(s8[8388608]{0:T(1024)(128)(4,1)} %bitcast.99), calls=%async_computation.5 | async-start | bytes 8388608
  612.8 390.4 %copy-start.4 = (f32[3]{0:T(128)S(1)}, f32[3]{0:T(128)}, u32[]{:S(2)}) copy-start(f32[3]{0:T(128)} %constant.195.clone) | copy-start | bytes 40
where the time goes:
time: 1010 us; the launch traced here: 1000 us
  local copies, waits for them, and re-layouts  329 us (33%)
  matrix products  282 us (28%)
  waiting for transfers between devices  244 us (24%)
  other arithmetic  87.5 us (9%)
  blocking collectives  41.8 us (4%)
  starting transfers between devices  13.1 us (1%)
    while x16, local copies, waits for them, and re-layouts  233 us
    dot_general x12, matrix products, product(): return jnp.einsum(form, left, right, precision=precise)  201 us
    ppermute x2, waiting for transfers between devices, partner(): lax.ppermute(array, axis, [(i, i ^ 1 << distance) for i in range(lax.axis...  137 us
    all_to_all x1, waiting for transfers between devices, on_device(): lax.all_to_all(slabs[0], 'rows', split_axis=1, concat_axis=0, tiled=True)  53.4 us
    all_to_all x1, waiting for transfers between devices, on_device(): lax.all_to_all(slabs[1], 'rows', split_axis=1, concat_axis=0, tiled=True)  53 us
    dot_general x8, matrix products, band_terms(): lax.dot_general(weighted, low_hot, (((1,), (1,)), ((), ())), preferred_el...  43.1 us
    psum x1, blocking collectives, on_device(): totals = lax.psum(slot * partial_sums[None], ('rows', 'rep'))  41.8 us
    add x2, local copies, waits for them, and re-layouts, complex_apply(): product(real_part, table_sin) + product(imag_part, table_cos)  23 us
  transfers between devices with their start and end apart: 4, of which 4 were waited for; matrix products, arithmetic and copies ran while one was open for 12% of the time, Pallas kernels for 0%

commit v1 on v0

--- a/solution.py
+++ b/solution.py
@@ -6,6 +6,28 @@
 
 NBINS = 1024
 precise = lax.Precision.HIGHEST
+
+
+def split_up(x, dim, length):
+    before, after = (x.shape[:dim], x.shape[dim + 1 :])
+    return jnp.moveaxis(x.reshape(*before, length, -1, *after), dim, 0)
+
+
+def laid_out(blocks, dim):
+    blocks = jnp.moveaxis(blocks, 0, dim)
+    dims = blocks.shape
+    return blocks.reshape(*dims[:dim], dims[dim] * dims[dim + 1], *dims[dim + 2 :])
+
+
+def swapped_with_each(shard, axis, split_dim, concat_dim):
+    length, index = (lax.axis_size(axis), lax.axis_index(axis))
+    pieces = split_up(shard, split_dim, length)
+    gathered = [pieces[index]]
+    for hop in range(1, length):
+        sent = pieces[index ^ hop]
+        gathered.append(lax.ppermute(sent, axis, [(i, i ^ hop) for i in range(length)]))
+    pieces = jnp.stack(gathered)[index ^ jnp.arange(length)]
+    return laid_out(pieces, concat_dim)
 
 
 def partner(array, axis, distance):
@@ -130,7 +152,7 @@
     spec_real, spec_imag = column_transform(
         (
             lax.all_to_all(slabs[0], "rows", split_axis=1, concat_axis=0, tiled=True),
-            lax.all_to_all(slabs[1], "rows", split_axis=1, concat_axis=0, tiled=True),
+            swapped_with_each(slabs[1], "rows", 1, 0),
         )
     )
     spec_real = spec_real.reshape(extent, columns)

time: 1010 us -> 1050 us (1.040)
  local copies, waits for them, and re-layouts: 329 us -> 364 us
    ppermute x0 -> x7, waiting for transfers between devices: none -> 99.4 us  [swapped_with_each(): lax.ppermute(sent, axis, [(i, i ^ hop) for i in range(length)])]
    all_to_all x1, waiting for transfers between devices: 53.4 us -> 0.01 us  [on_device(): lax.all_to_all(slabs[0], 'rows', split_axis=1, concat_axis=0, tiled=True)]
    all_to_all x1 -> x0, waiting for transfers between devices: 53 us -> none  [on_device(): lax.all_to_all(slabs[1], 'rows', split_axis=1, concat_axis=0, tiled=True)]
    another operation x0 -> x10, local copies, waits for them, and re-layouts: none -> 23.1 us
    unnamed x20 -> x29, local copies, waits for them, and re-layouts: 21.3 us -> 35 us
  transfers between devices with their start and end apart: 4 -> 10, of which waited for: 4 -> 6; matrix products, arithmetic and copies ran while one was open for 12% -> 14% of each run, Pallas kernels for 0% -> 0%
where the time goes in v1:
time: 1050 us; the launch traced here: 1040 us
  local copies, waits for them, and re-layouts  364 us (35%)
  matrix products  282 us (27%)
  waiting for transfers between devices  240 us (23%)
  other arithmetic  87.6 us (8%)
  blocking collectives  39.9 us (4%)
  starting transfers between devices  15.2 us (1%)
    while x16, local copies, waits for them, and re-layouts  233 us
    dot_general x12, matrix products, product(): return jnp.einsum(form, left, right, precision=precise)  200 us
    ppermute x2, waiting for transfers between devices, partner(): lax.ppermute(array, axis, [(i, i ^ 1 << distance) for i in range(lax.axis...  141 us
    ppermute x7, waiting for transfers between devices, swapped_with_each(): lax.ppermute(sent, axis, [(i, i ^ hop) for i in range(length)])  99.4 us
    dot_general x8, matrix products, band_terms(): lax.dot_general(weighted, low_hot, (((1,), (1,)), ((), ())), preferred_el...  43.1 us
    psum x1, blocking collectives, on_device(): totals = lax.psum(slot * partial_sums[None], ('rows', 'rep'))  39.9 us
    unnamed x29, local copies, waits for them, and re-layouts  35 us
    another operation x9, local copies, waits for them, and re-layouts  22 us
  transfers between devices with their start and end apart: 10, of which 6 were waited for; matrix products, arithmetic and copies ran while one was open for 14% of the time, Pallas kernels for 0%

profile of v1, /device:TPU:0, one launch (start us, length us, event | category | flops | bytes accessed | tf_op | source)
XLA Modules:
  0.0 1036.3 jit_solution(7703362448789414446)
XLA Ops:
  29.3 17.6 %fusion.37 = f32[64,512,64]{1,0,2:T(8,128)} fusion(f32[512,64,64]{0,2,1:T(8,128)} %bitcast.113), kind=kOutput, calls=%fused_computation.68 | convolution fusion | flops 1610674176 | bytes 16777216 | tf_op jit(solution)/shard_map/yan,ak->ykn/dot_general | solution.py:75
  46.9 21.0 %subtract_bitcast_fusion.1 = (f32[512,64,64]{0,1,2:T(8,128)S(1)}, f32[512,64,64]{0,1,2:T(8,128)}) fusion(f32[64,512,64]{1,0,2:T(8,128)} %fusion.37, f32[64,64]{0,1:T(8,128)S(1)} %get-tuple-element.253, f32[64,64]{0,1:T(8,128)S(1)} %get-tuple-element.254, f32[512,64,64]{0,2,1:T(8,128)} %bitcast.114), kind=kOutput, calls=%fused_computation.43 | convolution fusion | flops 1623252992 | bytes 33587200 | tf_op jit(solution)/shard_map/yan,ak->ykn/dot_general | solution.py:74
  67.9 19.3 %fusion.31 = f32[64,512,64]{1,0,2:T(8,128)S(1)} fusion(f32[512,64,64]{0,1,2:T(8,128)} %get-tuple-element.240), kind=kOutput, calls=%fused_computation.62 | convolution fusion | flops 1610674176 | bytes 16777216 | tf_op jit(solution)/shard_map/ykn,nm->ymk/dot_general | solution.py:52
  134.4 17.1 %add_bitcast_fusion = f32[512,64,64]{0,1,2:T(8,128)S(1)} fusion(f32[64,512,64]{1,0,2:T(8,128)S(1)} %fusion.29, f32[512,64,64]{0,1,2:T(8,128)} %copy-done), kind=kOutput, calls=%fused_computation.40 | convolution fusion | flops 1612771328 | bytes 25165824 | tf_op jit(solution)/shard_map/ykn,nm->ymk/dot_general | solution.py:52
  192.1 42.9 %collective-permute-done.1 = f32[512,1,512]{2,0,1:T(8,128)} collective-permute-done((f32[512,1,512]{2,0,1:T(8,128)}, f32[512,1,512]{2,0,1:T(8,128)}, u32[]{:S(2)}, u32[]{:S(2)}) %collective-permute-start.1) | collective-permute-done | bytes 1048608 | tf_op jit(solution)/shard_map/ppermute | solution.py:28
  237.3 18.5 %collective-permute-done.2 = f32[512,1,512]{2,0,1:T(8,128)} collective-permute-done((f32[512,1,512]{2,0,1:T(8,128)}, f32[512,1,512]{2,0,1:T(8,128)}, u32[]{:S(2)}, u32[]{:S(2)}) %collective-permute-start.2) | collective-permute-done | bytes 1048608 | tf_op jit(solution)/shard_map/ppermute | solution.py:28
  262.6 18.1 %collective-permute-done.5 = f32[512,1,512]{2,0,1:T(8,128)S(1)} collective-permute-done((f32[512,1,512]{2,0,1:T(8,128)}, f32[512,1,512]{2,0,1:T(8,128)S(1)}, u32[]{:S(2)}, u32[]{:S(2)}) %collective-permute-start.5) | collective-permute-done | bytes 1048608 | tf_op jit(solution)/shard_map/ppermute | solution.py:28
  281.8 19.9 %collective-permute-done.6 = f32[512,1,512]{2,0,1:T(8,128)S(1)} collective-permute-done((f32[512,1,512]{2,0,1:T(8,128)S(1)}, f32[512,1,512]{2,0,1:T(8,128)S(1)}, u32[]{:S(2)}, u32[]{:S(2)}) %collective-permute-start.6) | collective-permute-done | bytes 1048608 | tf_op jit(solution)/shard_map/ppermute | solution.py:28
  310.5 17.8 %fusion.23 = f32[64,64,512]{2,0,1:T(8,128)} fusion(f32[64,64,512]{2,1,0:T(8,128)} %bitcast.117), kind=kOutput, calls=%fused_computation.54 | convolution fusion | flops 1610674176 | bytes 16777216 | tf_op jit(solution)/shard_map/anbc,ak->knbc/dot_general | solution.py:52
  337.5 18.2 %fusion.25 = f32[64,64,512]{2,0,1:T(8,128)} fusion(f32[64,64,512]{2,1,0:T(8,128)} %bitcast.115), kind=kOutput, calls=%fused_computation.56 | convolution fusion | flops 1610674176 | bytes 16777216 | tf_op jit(solution)/shard_map/anbc,ak->knbc/dot_general | solution.py:52
  369.0 24.6 %multiply_subtract_fusion = (f32[64,64,512]{2,0,1:T(8,128)}, f32[64,64,512]{2,0,1:T(8,128)}) fusion(f32[64,64]{0,1:T(8,128)S(1)} %get-tuple-element.253, f32[64,64]{0,1:T(8,128)S(1)} %get-tuple-element.254, f32[64,64,512]{2,0,1:T(8,128)} %fusion.25, f32[64,64,512]{2,0,1:T(8,128)} %fusion.27, f32[64,64,512]{2,0,1:T(8,128)} %fusion.23, ...), kind=kOutput, calls=%fused_computation.39 | convolution fusion | flops 1627447296 | bytes 50364416 | tf_op jit(solution)/shard_map/anbc,ak->knbc/dot_general | solution.py:52
  393.6 18.5 %fusion.13 = f32[64,64,512]{2,0,1:T(8,128)} fusion(f32[64,64,512]{2,0,1:T(8,128)} %get-tuple-element.238), kind=kOutput, calls=%fused_computation.44 | convolution fusion | flops 1610670080 | bytes 16777216 | tf_op jit(solution)/shard_map/knbc,nm->mkbc/dot_general | solution.py:52
  491.2 59.4 %collective-permute-done.8 = f32[2048,512]{1,0:T(8,128)} collective-permute-done((f32[2048,512]{1,0:T(8,128)}, f32[2048,512]{1,0:T(8,128)}, u32[]{:S(2)}, u32[]{:S(2)}) %collective-permute-start.8) | collective-permute-done | bytes 4194336 | tf_op jit(solution)/shard_map/ppermute | solution.py:34
  558.7 81.4 %collective-permute-done.7 = f32[2048,512]{1,0:T(8,128)} collective-permute-done((f32[2048,512]{1,0:T(8,128)}, f32[2048,512]{1,0:T(8,128)}, u32[]{:S(2)}, u32[]{:S(2)}) %collective-permute-start.7) | collective-permute-done | bytes 4194336 | tf_op jit(solution)/shard_map/ppermute | solution.py:34
  646.8 348.4 %while.14 = (s32[]{:T(128)}, f32[3,1024]{1,0:T(4,128)S(1)}, s32[]{:T(128)}, s32[8]{0:T(128)S(1)}, s32[]{:T(128)}, /*index=5*/f32[8,256,512]{2,1,0:T(8,128)}, f32...) while((s32[]{:T(128)}, f32[3,1024]{1,0:T(4,128)S(1)}, ...), condition=%wide.region_1.2_spmd.clone, body=%wide.region_0.1_spmd.clone.sunk | while | flops 832713472 | bytes 68505800 | solution.py:197
  656.1 28.9 %copy.109 = bf16[6,8,256,512]{3,1,2,0:T(8,128)(2,1)S(1)} copy(bf16[6,8,256,512]{3,2,1,0:T(8,128)(2,1)S(1)} %bitcast.109) | data formatting | bytes 25165824 | tf_op jit(solution)/shard_map/while
  699.6 28.9 %copy.109 = bf16[6,8,256,512]{3,1,2,0:T(8,128)(2,1)S(1)} copy(bf16[6,8,256,512]{3,2,1,0:T(8,128)(2,1)S(1)} %bitcast.109) | data formatting | bytes 25165824 | tf_op jit(solution)/shard_map/while
  743.1 28.9 %copy.109 = bf16[6,8,256,512]{3,1,2,0:T(8,128)(2,1)S(1)} copy(bf16[6,8,256,512]{3,2,1,0:T(8,128)(2,1)S(1)} %bitcast.109) | data formatting | bytes 25165824 | tf_op jit(solution)/shard_map/while
  786.6 28.9 %copy.109 = bf16[6,8,256,512]{3,1,2,0:T(8,128)(2,1)S(1)} copy(bf16[6,8,256,512]{3,2,1,0:T(8,128)(2,1)S(1)} %bitcast.109) | data formatting | bytes 25165824 | tf_op jit(solution)/shard_map/while
  830.1 28.9 %copy.109 = bf16[6,8,256,512]{3,1,2,0:T(8,128)(2,1)S(1)} copy(bf16[6,8,256,512]{3,2,1,0:T(8,128)(2,1)S(1)} %bitcast.109) | data formatting | bytes 25165824 | tf_op jit(solution)/shard_map/while
  873.7 28.9 %copy.109 = bf16[6,8,256,512]{3,1,2,0:T(8,128)(2,1)S(1)} copy(bf16[6,8,256,512]{3,2,1,0:T(8,128)(2,1)S(1)} %bitcast.109) | data formatting | bytes 25165824 | tf_op jit(solution)/shard_map/while
  917.2 28.9 %copy.109 = bf16[6,8,256,512]{3,1,2,0:T(8,128)(2,1)S(1)} copy(bf16[6,8,256,512]{3,2,1,0:T(8,128)(2,1)S(1)} %bitcast.109) | data formatting | bytes 25165824 | tf_op jit(solution)/shard_map/while
  960.7 28.9 %copy.109 = bf16[6,8,256,512]{3,1,2,0:T(8,128)(2,1)S(1)} copy(bf16[6,8,256,512]{3,2,1,0:T(8,128)(2,1)S(1)} %bitcast.109) | data formatting | bytes 25165824 | tf_op jit(solution)/shard_map/while
  995.3 39.9 %psum.7 = f32[2,3,1024]{2,0,1:T(2,128)S(1)} all-reduce(f32[2,3,1024]{2,0,1:T(2,128)S(1)} %broadcast_multiply_fusion.2), channel_id=1, replica_groups=mesh['rows'=8,'rep'=4] {'rows','rep'}, use_global_device_ids=true, to_apply=%region_2.3 | all-reduce | flops 6144 | bytes 49152 | tf_op jit(solution)/shard_map/psum | solution.py:204
  (193 shorter events, 363.7 us)
Async XLA Ops:
  67.9 19.4 %copy-start = (f32[512,64,64]{0,1,2:T(8,128)}, f32[512,64,64]{0,1,2:T(8,128)S(1)}, u32[]{:S(2)}) copy-start(f32[512,64,64]{0,1,2:T(8,128)S(1)} %get-tuple-element.239) | copy-start | bytes 25165828
  112.4 216.0 %all-to-all-start = ((f32[512,8,512]{0,2,1:T(8,128)}), f32[512,8,512]{0,2,1:T(8,128)}, u32[]{:S(2)}, u32[]{:S(2)}) async-start(f32[512,8,512]{0,2,1:T(8,128)} %bitcast.120), calls=%async_computation | async-start | bytes 16777216 | tf_op jit(solution)/shard_map/all_to_all | solution.py:154
  168.5 18.8 %collective-permute-start = (f32[512,1,512]{2,0,1:T(8,128)}, f32[512,1,512]{2,0,1:T(8,128)}, u32[]{:S(2)}, u32[]{:S(2)}) collective-permute-start(f32[512,1,512]{2,0,1:T(8,128)} %bitcast.137), channel_id=1, source_target_pairs={{0,4},{4,0},{8,12},{12,8},{16,20},{20,16},{24,28},{28,24},{1,5},{5... | collective-permute-start | bytes 3145736 | tf_op jit(solution)/shard_map/ppermute | solution.py:28
  171.5 63.4 %collective-permute-start.1 = (f32[512,1,512]{2,0,1:T(8,128)}, f32[512,1,512]{2,0,1:T(8,128)}, u32[]{:S(2)}, u32[]{:S(2)}) collective-permute-start(f32[512,1,512]{2,0,1:T(8,128)} %bitcast.136), channel_id=1, source_target_pairs={{0,8},{4,12},{8,0},{12,4},{16,24},{20,28},{24,16},{28,20},{1,9},{5... | collective-permute-start | bytes 3145736 | tf_op jit(solution)/shard_map/ppermute | solution.py:28
  176.2 79.6 %collective-permute-start.2 = (f32[512,1,512]{2,0,1:T(8,128)}, f32[512,1,512]{2,0,1:T(8,128)}, u32[]{:S(2)}, u32[]{:S(2)}) collective-permute-start(f32[512,1,512]{2,0,1:T(8,128)} %bitcast.135), channel_id=1, source_target_pairs={{0,12},{4,8},{8,4},{12,0},{16,28},{20,24},{24,20},{28,16},{1,13},{... | collective-permute-start | bytes 3145736 | tf_op jit(solution)/shard_map/ppermute | solution.py:28
  178.8 79.2 %collective-permute-start.3 = (f32[512,1,512]{2,0,1:T(8,128)}, f32[512,1,512]{2,0,1:T(8,128)}, u32[]{:S(2)}, u32[]{:S(2)}) collective-permute-start(f32[512,1,512]{2,0,1:T(8,128)} %bitcast.134), channel_id=1, source_target_pairs={{0,16},{4,20},{8,24},{12,28},{16,0},{20,4},{24,8},{28,12},{1,17},{... | collective-permute-start | bytes 3145736 | tf_op jit(solution)/shard_map/ppermute | solution.py:28
  183.1 77.2 %collective-permute-start.4 = (f32[512,1,512]{2,0,1:T(8,128)}, f32[512,1,512]{2,0,1:T(8,128)}, u32[]{:S(2)}, u32[]{:S(2)}) collective-permute-start(f32[512,1,512]{2,0,1:T(8,128)} %bitcast.133), channel_id=1, source_target_pairs={{0,20},{4,16},{8,28},{12,24},{16,4},{20,0},{24,12},{28,8},{1,21},{... | collective-permute-start | bytes 3145736 | tf_op jit(solution)/shard_map/ppermute | solution.py:28
  184.5 50.5 %copy-start.4 = (f32[512,1,1,512]{3,0,2,1:T(8,128)S(1)}, f32[512,1,1,512]{3,0,2,1:T(8,128)}, u32[]{:S(2)}) copy-start(f32[512,1,1,512]{3,0,2,1:T(8,128)} %copy.55) | copy-start | bytes 3145732
  187.3 93.4 %collective-permute-start.5 = (f32[512,1,512]{2,0,1:T(8,128)}, f32[512,1,512]{2,0,1:T(8,128)S(1)}, u32[]{:S(2)}, u32[]{:S(2)}) collective-permute-start(f32[512,1,512]{2,0,1:T(8,128)} %bitcast.139), channel_id=1, source_target_pairs={{0,24},{4,28},{8,16},{12,20},{16,8},{20,12},{24,0},{28,4},{1,25},{... | collective-permute-start | bytes 3145736 | tf_op jit(solution)/shard_map/ppermute | solution.py:28
  235.0 66.8 %collective-permute-start.6 = (f32[512,1,512]{2,0,1:T(8,128)S(1)}, f32[512,1,512]{2,0,1:T(8,128)S(1)}, u32[]{:S(2)}, u32[]{:S(2)}) collective-permute-start(f32[512,1,512]{2,0,1:T(8,128)S(1)} %bitcast.138), channel_id=1, source_target_pairs={{0,28},{4,24},{8,20},{12,16},{16,12},{20,8},{24,4},{28,0},{1,29},{... | collective-permute-start | bytes 3145736 | tf_op jit(solution)/shard_map/ppermute | solution.py:28
  337.5 18.2 %copy-start.1 = (f32[8,512,1,512]{3,1,0,2:T(8,128)S(1)}, f32[8,512,1,512]{3,1,0,2:T(8,128)}, u32[]{:S(2)}) copy-start(f32[8,512,1,512]{3,1,0,2:T(8,128)} %copy.43) | copy-start | bytes 25165828
  393.6 18.5 %copy-start.2 = (f32[64,64,512]{2,0,1:T(8,128)S(1)}, f32[64,64,512]{2,0,1:T(8,128)}, u32[]{:S(2)}) copy-start(f32[64,64,512]{2,0,1:T(8,128)} %get-tuple-element.238) | copy-start | bytes 25165828
  393.6 31.0 %slice-start = ((s8[8388608]{0:T(1024)(128)(4,1)}), s8[4194304]{0:T(1024)(128)(4,1)S(1)}, s32[]{:S(2)}) async-start(s8[8388608]{0:T(1024)(128)(4,1)} %bitcast.111), calls=%async_computation.1 | async-start | bytes 8388608
  412.1 12.5 %slice-start.1 = ((s8[8388608]{0:T(1024)(128)(4,1)}), s8[4194304]{0:T(1024)(128)(4,1)S(1)}, s32[]{:S(2)}) async-start(s8[8388608]{0:T(1024)(128)(4,1)} %bitcast.111), calls=%async_computation.2 | async-start | bytes 8388608
  456.4 94.2 %collective-permute-start.8 = (f32[2048,512]{1,0:T(8,128)}, f32[2048,512]{1,0:T(8,128)}, u32[]{:S(2)}, u32[]{:S(2)}) collective-permute-start(f32[2048,512]{1,0:T(8,128)} %constant_dynamic-slice_fusion.1), channel_id=1, source_target_pairs={{0,1},{1,0},{2,3},{3,2},{4,5},{5,4},{6,7},{7,6},{8,9},{9,8},{10,11... | collective-permute-start | bytes 12582920 | tf_op jit(solution)/shard_map/ppermute | solution.py:34
  480.7 3.2 copy-start.3
  486.4 153.8 %collective-permute-start.7 = (f32[2048,512]{1,0:T(8,128)}, f32[2048,512]{1,0:T(8,128)}, u32[]{:S(2)}, u32[]{:S(2)}) collective-permute-start(f32[2048,512]{1,0:T(8,128)} %constant_dynamic-slice_fusion.2), channel_id=1, source_target_pairs={{0,1},{1,0},{2,3},{3,2},{4,5},{5,4},{6,7},{7,6},{8,9},{9,8},{10,11... | collective-permute-start | bytes 12582920 | tf_op jit(solution)/shard_map/ppermute | solution.py:34
  486.4 153.7 %slice-start.2 = ((s8[8388608]{0:T(1024)(128)(4,1)}), s8[4194304]{0:T(1024)(128)(4,1)S(1)}, s32[]{:S(2)}) async-start(s8[8388608]{0:T(1024)(128)(4,1)} %bitcast.124), calls=%async_computation.3 | async-start | bytes 8388608
  491.2 149.0 %slice-start.3 = ((s8[8388608]{0:T(1024)(128)(4,1)}), s8[4194304]{0:T(1024)(128)(4,1)S(1)}, s32[]{:S(2)}) async-start(s8[8388608]{0:T(1024)(128)(4,1)} %bitcast.124), calls=%async_computation.4 | async-start | bytes 8388608
  646.8 388.3 %copy-start.5 = (f32[3]{0:T(128)S(1)}, f32[3]{0:T(128)}, u32[]{:S(2)}) copy-start(f32[3]{0:T(128)} %constant.209.clone) | copy-start | bytes 40
